TPU v7x, 32 devices: a whole 2x2x4 slice. The times are simulated.
32 devices in a mesh: gx: 8 (over z, x), gy: 4 (over y, core).
Axes of the slice: x: 2, y: 2, z: 4, core: 2. Of those that a mesh axis runs over, the one named last changes fastest.
Arguments:
- right_side: float32 [8, 32, 64, 512], P(None, 'gx', 'gy'), may hold values from -6 to 6
- velocity: float32 [3, 32, 64, 512], P(None, 'gx', 'gy'), may hold values from -0.5 to 0.5
- reaction: float32 [32, 64, 512], P('gx', 'gy'), may hold values from 0.1 to 2
Outputs:
- solution: float32 [8, 32, 64, 512], P(None, 'gx', 'gy')
- residual: float32 [8, 32, 64, 512], P(None, 'gx', 'gy')
All inputs are finite; a program needn't handle non-finite values.
Results may differ from a plain program's by a relative error of at most 0.00045.
Values sent between devices are 32-bit elements; how exact they have to be, the bound alone decides.
A program may use at most 64 MiB of HBM per device.

v0:
```python
import functools

import jax
import jax.numpy as jnp
from jax import lax
from jax.experimental import pallas as pl
from jax.experimental.pallas import tpu as pltpu
from jax.sharding import PartitionSpec as P

S = 4
ITERS = 2
F32 = jnp.float32
BF16 = jnp.bfloat16
MESH = pl.DeviceIdType.MESH


def iota(shape, dim):
    return lax.broadcasted_iota(jnp.int32, shape, dim)


def split(value):
    high = value.astype(BF16)
    low = (value - high.astype(F32)).astype(BF16)
    return jnp.concatenate([high, low], axis=0)


def coefficients(gram):
    size = S * 8
    lane = iota((size, 128), 1)
    row = iota((size, 128), 0)
    mixed = 6.0 * (gram[:size] + gram[8:])
    normal = 6.0 * (mixed + pltpu.roll(mixed, 120, 1))
    target = pltpu.roll(mixed, size, 1)
    work = jnp.where(lane < size, normal, jnp.where(lane < size + 8, target, 0.0))
    for k in range(size):
        pivot = 1.0 / work[k : k + 1, k : k + 1]
        line = work[k : k + 1, :] * pivot
        column = work[:, k : k + 1]
        work = jnp.where(row == k, line, work - column * line)
    update = jnp.where(lane < 8, pltpu.roll(work, 128 - size, 1), 0.0)
    none = jnp.zeros((8, 128), F32)
    upper = jnp.concatenate([update, none], axis=0)
    lower = jnp.concatenate([none, update], axis=0)
    total = size + 8
    start = jnp.where((iota((total, 128), 0) == iota((total, 128), 1)) & (iota((total, 128), 1) < 8), 1.0, 0.0)
    rest = start - 6.0 * (upper + lower)
    return upper + pltpu.roll(rest, 8, 1)


def kernel(ngx, ngy, X, Y, Z, rhs_ref, cf_ref, sol_ref, res_ref, basis, parts, gs, ag, ar_y, ar_x, send, recv, sy_s, sy_r, sx_s, sx_r):
    ix = lax.axis_index("gx")
    iy = lax.axis_index("gy")
    sides = [
        (ix > 0, ix - 1, iy),
        (ix < ngx - 1, ix + 1, iy),
        (iy > 0, ix, iy - 1),
        (iy < ngy - 1, ix, iy + 1),
    ]

    def face(slot, side):
        return [
            basis.at[slot, 1, pl.ds(1, Y)],
            basis.at[slot, X, pl.ds(1, Y)],
            basis.at[slot, pl.ds(1, X), 1],
            basis.at[slot, pl.ds(1, X), Y],
        ][side]

    def halo(slot, side):
        return [
            basis.at[slot, 0, pl.ds(1, Y)],
            basis.at[slot, X + 1, pl.ds(1, Y)],
            basis.at[slot, pl.ds(1, X), 0],
            basis.at[slot, pl.ds(1, X), Y + 1],
        ][side]

    def copy(slot, side):
        return pltpu.make_async_remote_copy(
            src_ref=face(slot, side),
            dst_ref=halo(slot, side ^ 1),
            send_sem=send.at[slot, side],
            recv_sem=recv.at[slot, side ^ 1],
            device_id={"gx": sides[side][1], "gy": sides[side][2]},
            device_id_type=MESH,
        )

    def start_sends(slot):
        for side in range(4):
            @pl.when(sides[side][0])
            def _():
                copy(slot, side).start()

    def wait_recvs(slot):
        for side in range(4):
            @pl.when(sides[side][0])
            def _():
                pltpu.make_async_remote_copy(
                    src_ref=halo(slot, side),
                    dst_ref=halo(slot, side),
                    send_sem=send.at[slot, side],
                    recv_sem=recv.at[slot, side],
                    device_id={"gx": sides[side][1], "gy": sides[side][2]},
                    device_id_type=MESH,
                ).wait_recv()

    def wait_sends(slot):
        for side in range(4):
            @pl.when(sides[side][0])
            def _():
                copy(slot, side).wait_send()

    nslots = ITERS * (S + 1)

    @pl.loop(0, nslots)
    def _(slot):
        for side in range(4):
            @pl.when(jnp.logical_not(sides[side][0]))
            def _():
                @pl.loop(0, Y if side < 2 else X)
                def _(at):
                    where = [(0, at + 1), (X + 1, at + 1), (at + 1, 0), (at + 1, Y + 1)][side]
                    basis[slot, where[0], where[1]] = jnp.zeros((8, Z), F32)

    lane = iota((8, Z), 1)
    first = lane == 0
    last = lane == Z - 1

    def keep(slot, power, x, y, value):
        basis[slot, x, y] = value
        parts[(x - 1) * Y + y - 1, pl.ds(16 * power, 16)] = split(value)

    def site(slot, power, x, y):
        c = basis[slot, x, y]
        xp, xm = basis[slot, x + 1, y], basis[slot, x - 1, y]
        yp, ym = basis[slot, x, y + 1], basis[slot, x, y - 1]
        zp = jnp.where(last, 0.0, pltpu.roll(c, Z - 1, 1))
        zm = jnp.where(first, 0.0, pltpu.roll(c, 1, 1))
        cf = [cf_ref[x - 1, y - 1, d : d + 1, :] for d in range(4)]
        sums = (xp + xm) - cf[0] * (xp - xm)
        sums = sums + ((yp + ym) - cf[1] * (yp - ym))
        sums = sums + ((zp + zm) - cf[2] * (zp - zm))
        keep(slot + 1, power + 1, x, y, (cf[3] * c - sums) * (1.0 / 6.0))

    def inner(slot, power):
        @pl.loop(2, X)
        def _(x):
            @pl.loop(2, Y)
            def _(y):
                site(slot, power, x, y)

    def outer(slot, power):
        @pl.loop(1, Y + 1)
        def _(y):
            site(slot, power, 1, y)
            site(slot, power, X, y)

        @pl.loop(2, X)
        def _(x):
            site(slot, power, x, 1)
            site(slot, power, x, Y)

    def exchange(outer_step, axis, count, me, buf, send_sem, recv_sem):
        def to(d):
            there = lax.rem(me + d, count)
            return pltpu.make_async_remote_copy(
                src_ref=ag.at[outer_step, axis],
                dst_ref=buf.at[outer_step, me],
                send_sem=send_sem.at[outer_step, d],
                recv_sem=recv_sem.at[outer_step, me],
                device_id={("gy", "gx")[axis]: there},
                device_id_type=MESH,
            )

        for d in range(1, count):
            to(d).start()
        for d in range(1, count):
            source = lax.rem(me + d, count)
            pltpu.make_async_remote_copy(
                src_ref=ag.at[outer_step, axis],
                dst_ref=buf.at[outer_step, source],
                send_sem=send_sem.at[outer_step, d],
                recv_sem=recv_sem.at[outer_step, source],
                device_id={("gy", "gx")[axis]: source},
                device_id_type=MESH,
            ).wait_recv()
        buf[outer_step, me] = ag[outer_step, axis]
        total = buf[outer_step, 0]
        for at in range(1, count):
            total = total + buf[outer_step, at]
        for d in range(1, count):
            to(d).wait_send()
        return total

    def gram_of(outer_step):
        def add(at, total):
            block = parts[at]
            return total + lax.dot_general(block, block, (((1,), (1,)), ((), ())), preferred_element_type=F32)

        gs[...] = jnp.zeros_like(gs)
        gs[:, 0:80] = lax.fori_loop(0, X * Y, add, jnp.zeros((80, 80), F32))
        rows = jnp.concatenate([gs[16 * j : 16 * j + 8, :] + gs[16 * j + 8 : 16 * j + 16, :] for j in range(S + 1)], axis=0)
        lanes = iota((40, 128), 1)
        gram = jnp.zeros((40, 128), F32)
        both = rows + pltpu.roll(rows, 120, 1)
        for j in range(S + 1):
            moved = both if j == 0 else pltpu.roll(both, 128 - 8 * j, 1)
            gram = jnp.where((lanes >= 8 * j) & (lanes < 8 * j + 8), moved, gram)
        tail = jnp.concatenate([gram[32:40], jnp.zeros((8, 128), F32)], axis=0)
        ag[outer_step, 0] = gram[0:16] + pltpu.roll(gram[16:32], 40, 1) + pltpu.roll(tail, 80, 1)
        ag[outer_step, 1] = exchange(outer_step, 0, ngy, iy, ar_y, sy_s, sy_r)
        total = exchange(outer_step, 1, ngx, ix, ar_x, sx_s, sx_r)
        gram = jnp.concatenate([total, pltpu.roll(total, 88, 1), pltpu.roll(total, 48, 1)[:8]], axis=0)
        return jnp.where(lanes < 40, gram, 0.0)

    @pl.loop(0, X)
    def _(x):
        @pl.loop(0, Y)
        def _(y):
            keep(0, 0, x + 1, y + 1, rhs_ref[x, y])

    for outer_step in range(ITERS):
        base = outer_step * (S + 1)

        @pl.loop(0, S)
        def _(power):
            slot = base + power
            start_sends(slot)
            inner(slot, power)
            wait_recvs(slot)
            outer(slot, power)
            wait_sends(slot)

        coefs = coefficients(gram_of(outer_step))
        doubled = []
        for j in range(S + 1):
            doubled += [coefs[8 * j : 8 * j + 8], coefs[8 * j : 8 * j + 8]]
        doubled.append(jnp.zeros((48, 128), F32))
        turned = jnp.concatenate(doubled, axis=0).T
        left = split(turned[0:16])[:, 0:80]

        @pl.loop(0, X)
        def _(x):
            @pl.loop(0, Y)
            def _(y):
                both = jnp.dot(left, parts[x * Y + y], preferred_element_type=F32)
                sol = both[0:8] + both[16:24]
                res = both[8:16] + both[24:32]
                if outer_step == 0:
                    sol_ref[x, y] = sol
                else:
                    sol_ref[x, y] += sol
                if outer_step < ITERS - 1:
                    keep(base + S + 1, 0, x + 1, y + 1, res)
                else:
                    res_ref[x, y] = res


def local(ngx, ngy, right_side, velocity, reaction):
    nrhs, X, Y, Z = right_side.shape
    rhs = jnp.transpose(right_side, (1, 2, 0, 3))
    cf = jnp.transpose(jnp.concatenate([velocity, reaction[None]], axis=0), (1, 2, 0, 3))
    nslots = ITERS * (S + 1)
    vmem = pl.BlockSpec(memory_space=pltpu.VMEM)
    out = jax.ShapeDtypeStruct((X, Y, nrhs, Z), F32)
    sol, res = pl.pallas_call(
        functools.partial(kernel, ngx, ngy, X, Y, Z),
        out_shape=(out, out),
        in_specs=[vmem, vmem],
        out_specs=(vmem, vmem),
        scratch_shapes=[
            pltpu.VMEM((nslots, X + 2, Y + 2, nrhs, Z), F32),
            pltpu.VMEM((X * Y, 80, Z), BF16),
            pltpu.VMEM((80, 128), F32),
            pltpu.VMEM((ITERS, 2, 16, 128), F32),
            pltpu.VMEM((ITERS, ngy, 16, 128), F32),
            pltpu.VMEM((ITERS, ngx, 16, 128), F32),
            pltpu.SemaphoreType.DMA((nslots, 4)),
            pltpu.SemaphoreType.DMA((nslots, 4)),
            pltpu.SemaphoreType.DMA((ITERS, ngy)),
            pltpu.SemaphoreType.DMA((ITERS, ngy)),
            pltpu.SemaphoreType.DMA((ITERS, ngx)),
            pltpu.SemaphoreType.DMA((ITERS, ngx)),
        ],
        compiler_params=pltpu.CompilerParams(has_side_effects=True, vmem_limit_bytes=56 * 1024 * 1024),
    )(rhs, cf)
    return jnp.transpose(sol, (2, 0, 1, 3)), jnp.transpose(res, (2, 0, 1, 3))


def solution(mesh):
    in_specs = (P(None, "gx", "gy", None), P(None, "gx", "gy", None), P("gx", "gy", None))
    out_specs = (P(None, "gx", "gy", None), P(None, "gx", "gy", None))
    body = functools.partial(local, mesh.shape["gx"], mesh.shape["gy"])
    return jax.shard_map(body, mesh=mesh, in_specs=in_specs, out_specs=out_specs, check_vma=False)
```

profile of v0, /device:TPU:0, one launch (start us, length us, event | category | flops | bytes accessed | tf_op | source)
XLA Modules:
  0.0 196.4 jit_solution(651301868897926476)
XLA Ops:
  0.6 1.0 broadcast_in_dim.3
  1.6 0.0 copy-start
  1.6 1.4 copy.6
  3.0 1.0 maximum_bitcast_fusion.cf_ref
  4.0 0.0 copy-done
  4.0 1.6 copy.10
  5.6 186.3 %shard_map.50 = (f32[4,16,8,512]{3,2,1,0:T(8,128)}, f32[4,16,8,512]{3,2,1,0:T(8,128)}) custom-call(f32[4,16,8,512]{3,2,1,0:T(8,128)} %bitcast.7, f32[4,16,4,512]{3,2,1,0:T(4,128)} %maximum_bitcast_fusion.cf_ref), custom_call_target="tpu_custom_call" | custom-call | tf_op jit(solution)/shard_map/pallas_call | solution.py:264
  191.9 0.0 copy-start.1
  191.9 2.9 %copy.7 = f32[8,4,16,512]{3,2,1,0:T(8,128)} copy(f32[8,4,16,512]{3,0,2,1:T(8,128)} %bitcast.9) | data formatting | bytes 2097152
  194.8 0.0 copy-done.1
  194.8 1.6 copy.8
Async XLA Ops:
  1.6 2.4 %copy-start = (f32[8,4,16,512]{3,2,1,0:T(8,128)S(1)}, f32[8,4,16,512]{3,2,1,0:T(8,128)}, u32[]{:S(2)}) copy-start(f32[8,4,16,512]{3,2,1,0:T(8,128)} %param.3) | copy-start | bytes 3145732
  191.9 2.9 %copy-start.1 = (f32[4,16,8,512]{3,2,1,0:T(8,128)S(1)}, f32[4,16,8,512]{3,2,1,0:T(8,128)}, u32[]{:S(2)}) copy-start(f32[4,16,8,512]{3,2,1,0:T(8,128)} %get-tuple-element.5) | copy-start | bytes 3145732
where the time goes:
time: 197 us; the launch traced here: 196 us
  Pallas kernels  186 us (94%)
  local copies, waits for them, and re-layouts  8.42 us (4%)
    pallas_call x1, Pallas kernels, local(): pl.pallas_call(functools.partial(kernel, ngx, ngy, X, Y, Z), out_shape=(o...  186 us
    unnamed x8, local copies, waits for them, and re-layouts  7.42 us

commit v1 on v0

--- a/solution.py
+++ b/solution.py
@@ -47,15 +47,70 @@
     return upper + pltpu.roll(rest, 8, 1)
 
 
-def kernel(ngx, ngy, X, Y, Z, rhs_ref, cf_ref, sol_ref, res_ref, basis, parts, gs, ag, ar_y, ar_x, send, recv, sy_s, sy_r, sx_s, sx_r):
+def kernel(ngx, ngy, X1, Y1, Z, rhs_ref, cf1_ref, sol_ref, res_ref, cf_ref, acc, turn_s, turn_r, back_s, back_r, basis, parts, gs, ag, ar_y, ar_x, send, recv, sy_s, sy_r, sx_s, sx_r):
     ix = lax.axis_index("gx")
     iy = lax.axis_index("gy")
+    X, Y = 2 * X1, Y1 // 2
+    odd = lax.rem(ix, 2)
+    partner = ix + 1 - 2 * odd
+    half = lax.rem(ix + iy, 2)
+    upper = half == 1
+    mine, theirs = odd * X1, (1 - odd) * X1
     sides = [
-        (ix > 0, ix - 1, iy),
-        (ix < ngx - 1, ix + 1, iy),
-        (iy > 0, ix, iy - 1),
-        (iy < ngy - 1, ix, iy + 1),
+        (ix > 1, ix - 2, iy),
+        (ix < ngx - 2, ix + 2, iy),
+        (upper | (iy > 0), jnp.where(upper, partner, ix), jnp.where(upper, iy, iy - 1)),
+        (jnp.logical_not(upper) | (iy < ngy - 1), jnp.where(upper, ix, partner), jnp.where(upper, iy + 1, iy)),
     ]
+
+    def swap(which):
+        source, target = [
+            (rhs_ref.at[:, pl.ds((1 - half) * Y, Y)], basis.at[0, pl.ds(1 + mine, X1), pl.ds(1, Y)]),
+            (cf1_ref.at[:, pl.ds((1 - half) * Y, Y)], cf_ref.at[pl.ds(mine, X1)]),
+        ][which]
+        return pltpu.make_async_remote_copy(
+            src_ref=source,
+            dst_ref=target,
+            send_sem=turn_s.at[which],
+            recv_sem=turn_r.at[which],
+            device_id={"gx": partner, "gy": iy},
+            device_id_type=MESH,
+        )
+
+    def swapped(which):
+        target = [basis.at[0, pl.ds(1 + theirs, X1), pl.ds(1, Y)], cf_ref.at[pl.ds(theirs, X1)]][which]
+        pltpu.make_async_remote_copy(
+            src_ref=target,
+            dst_ref=target,
+            send_sem=turn_s.at[which],
+            recv_sem=turn_r.at[which],
+            device_id={"gx": partner, "gy": iy},
+            device_id_type=MESH,
+        ).wait_recv()
+
+    def back(which, plane):
+        return pltpu.make_async_remote_copy(
+            src_ref=acc.at[which, theirs + plane],
+            dst_ref=[sol_ref, res_ref][which].at[plane, pl.ds(half * Y, Y)],
+            send_sem=back_s.at[which, plane],
+            recv_sem=back_r.at[which, plane],
+            device_id={"gx": partner, "gy": iy},
+            device_id_type=MESH,
+        )
+
+    def came_back(which, plane):
+        target = [sol_ref, res_ref][which].at[plane, pl.ds((1 - half) * Y, Y)]
+        pltpu.make_async_remote_copy(
+            src_ref=target,
+            dst_ref=target,
+            send_sem=back_s.at[which, plane],
+            recv_sem=back_r.at[which, plane],
+            device_id={"gx": partner, "gy": iy},
+            device_id_type=MESH,
+        ).wait_recv()
+
+    swap(0).start()
+    swap(1).start()
 
     def face(slot, side):
         return [
@@ -143,17 +198,17 @@
     def inner(slot, power):
         @pl.loop(2, X)
         def _(x):
-            @pl.loop(2, Y)
+            @pl.loop(2, Y, unroll=True)
             def _(y):
                 site(slot, power, x, y)
 
     def outer(slot, power):
-        @pl.loop(1, Y + 1)
+        @pl.loop(1, Y + 1, unroll=4)
         def _(y):
             site(slot, power, 1, y)
             site(slot, power, X, y)
 
-        @pl.loop(2, X)
+        @pl.loop(2, X, unroll=True)
         def _(x):
             site(slot, power, x, 1)
             site(slot, power, x, Y)
@@ -196,7 +251,7 @@
             return total + lax.dot_general(block, block, (((1,), (1,)), ((), ())), preferred_element_type=F32)
 
         gs[...] = jnp.zeros_like(gs)
-        gs[:, 0:80] = lax.fori_loop(0, X * Y, add, jnp.zeros((80, 80), F32))
+        gs[:, 0:80] = lax.fori_loop(0, X * Y, add, jnp.zeros((80, 80), F32), unroll=8)
         rows = jnp.concatenate([gs[16 * j : 16 * j + 8, :] + gs[16 * j + 8 : 16 * j + 16, :] for j in range(S + 1)], axis=0)
         lanes = iota((40, 128), 1)
         gram = jnp.zeros((40, 128), F32)
@@ -211,11 +266,21 @@
         gram = jnp.concatenate([total, pltpu.roll(total, 88, 1), pltpu.roll(total, 48, 1)[:8]], axis=0)
         return jnp.where(lanes < 40, gram, 0.0)
 
-    @pl.loop(0, X)
+    @pl.loop(0, X1)
     def _(x):
-        @pl.loop(0, Y)
+        @pl.loop(0, Y, unroll=8)
         def _(y):
-            keep(0, 0, x + 1, y + 1, rhs_ref[x, y])
+            keep(0, 0, mine + x + 1, y + 1, rhs_ref[x, half * Y + y])
+            cf_ref[mine + x, y] = cf1_ref[x, half * Y + y]
+
+    swapped(0)
+
+    def split_swapped():
+        @pl.loop(0, X1)
+        def _(x):
+            @pl.loop(0, Y, unroll=8)
+            def _(y):
+                parts[(theirs + x) * Y + y, pl.ds(0, 16)] = split(basis[0, theirs + x + 1, y + 1])
 
     for outer_step in range(ITERS):
         base = outer_step * (S + 1)
@@ -224,6 +289,11 @@
         def _(power):
             slot = base + power
             start_sends(slot)
+            if outer_step == 0:
+                @pl.when(power == 0)
+                def _():
+                    split_swapped()
+                    swapped(1)
             inner(slot, power)
             wait_recvs(slot)
             outer(slot, power)
@@ -237,21 +307,45 @@
         turned = jnp.concatenate(doubled, axis=0).T
         left = split(turned[0:16])[:, 0:80]
 
-        @pl.loop(0, X)
-        def _(x):
-            @pl.loop(0, Y)
-            def _(y):
-                both = jnp.dot(left, parts[x * Y + y], preferred_element_type=F32)
-                sol = both[0:8] + both[16:24]
-                res = both[8:16] + both[24:32]
-                if outer_step == 0:
-                    sol_ref[x, y] = sol
-                else:
-                    sol_ref[x, y] += sol
-                if outer_step < ITERS - 1:
+        def combined(x, y):
+            both = jnp.dot(left, parts[x * Y + y], preferred_element_type=F32)
+            sol, res = both[0:8] + both[16:24], both[8:16] + both[24:32]
+            return sol if outer_step == 0 else acc[0, x, y] + sol, res
+
+        if outer_step < ITERS - 1:
+            @pl.loop(0, X)
+            def _(x):
+                @pl.loop(0, Y, unroll=8)
+                def _(y):
+                    sol, res = combined(x, y)
+                    acc[0, x, y] = sol
                     keep(base + S + 1, 0, x + 1, y + 1, res)
-                else:
-                    res_ref[x, y] = res
+        else:
+            @pl.loop(0, X1)
+            def _(x):
+                @pl.loop(0, Y, unroll=8)
+                def _(y):
+                    acc[0, theirs + x, y], acc[1, theirs + x, y] = combined(theirs + x, y)
+
+                back(0, x).start()
+                back(1, x).start()
+
+            @pl.loop(0, X1)
+            def _(x):
+                @pl.loop(0, Y, unroll=8)
+                def _(y):
+                    sol, res = combined(mine + x, y)
+                    sol_ref[x, half * Y + y] = sol
+                    res_ref[x, half * Y + y] = res
+
+            for which in range(2):
+                swap(which).wait_send()
+
+            @pl.loop(0, X1)
+            def _(x):
+                for which in range(2):
+                    came_back(which, x)
+                    back(which, x).wait_send()
 
 
 def local(ngx, ngy, right_side, velocity, reaction):
@@ -267,7 +361,13 @@
         in_specs=[vmem, vmem],
         out_specs=(vmem, vmem),
         scratch_shapes=[
-            pltpu.VMEM((nslots, X + 2, Y + 2, nrhs, Z), F32),
+            pltpu.VMEM((2 * X, Y // 2, 4, Z), F32),
+            pltpu.VMEM((2, 2 * X, Y // 2, nrhs, Z), F32),
+            pltpu.SemaphoreType.DMA((2,)),
+            pltpu.SemaphoreType.DMA((2,)),
+            pltpu.SemaphoreType.DMA((2, X)),
+            pltpu.SemaphoreType.DMA((2, X)),
+            pltpu.VMEM((nslots, 2 * X + 2, Y // 2 + 2, nrhs, Z), F32),
             pltpu.VMEM((X * Y, 80, Z), BF16),
             pltpu.VMEM((80, 128), F32),
             pltpu.VMEM((ITERS, 2, 16, 128), F32),

time: 197 us -> 131 us (0.66)
  Pallas kernels: 186 us -> 120 us
    pallas_call x1, Pallas kernels: 186 us -> 120 us  [local(): pl.pallas_call(functools.partial(kernel, ngx, ngy, X, Y, Z), out_shape=(o...]
where the time goes in v1:
time: 131 us; the launch traced here: 130 us
  Pallas kernels  120 us (92%)
  local copies, waits for them, and re-layouts  8.42 us (6%)
    pallas_call x1, Pallas kernels, local(): pl.pallas_call(functools.partial(kernel, ngx, ngy, X, Y, Z), out_shape=(o...  120 us
    unnamed x8, local copies, waits for them, and re-layouts  7.42 us

profile of v1, /device:TPU:0, one launch (start us, length us, event | category | flops | bytes accessed | tf_op | source)
XLA Modules:
  0.0 130.5 jit_solution(15590122967658971579)
XLA Ops:
  0.6 1.0 broadcast_in_dim.3
  1.6 0.0 copy-start
  1.6 1.4 %copy.6 = f32[3,4,16,512]{3,0,2,1:T(4,128)S(1)} copy(f32[3,4,16,512]{3,2,1,0:T(8,128)} %param.4) | data formatting | bytes 786432 | tf_op args[1]
  3.0 1.0 maximum_bitcast_fusion.cf1_ref
  4.0 0.0 copy-done
  4.0 1.6 %copy.10 = f32[8,4,16,512]{3,0,2,1:T(8,128)} copy(f32[8,4,16,512]{3,2,1,0:T(8,128)S(1)} %copy-done) | data formatting | bytes 2097152 | tf_op args[0]
  5.6 120.4 %shard_map.50 = (f32[4,16,8,512]{3,2,1,0:T(8,128)}, f32[4,16,8,512]{3,2,1,0:T(8,128)}) custom-call(f32[4,16,8,512]{3,2,1,0:T(8,128)} %bitcast.7, f32[4,16,4,512]{3,2,1,0:T(4,128)} %maximum_bitcast_fusion.cf1_ref), custom_call_target="tpu_custom_call" | custom-call | tf_op jit(solution)/shard_map/pallas_call | solution.py:358
  126.0 0.0 copy-start.1
  126.0 2.9 %copy.7 = f32[8,4,16,512]{3,2,1,0:T(8,128)} copy(f32[8,4,16,512]{3,0,2,1:T(8,128)} %bitcast.9) | data formatting | bytes 2097152
  128.9 0.0 copy-done.1
  128.9 1.6 %copy.8 = f32[8,4,16,512]{3,2,1,0:T(8,128)} copy(f32[8,4,16,512]{3,0,2,1:T(8,128)S(1)} %bitcast.8) | data formatting | bytes 2097152
Async XLA Ops:
  1.6 2.4 %copy-start = (f32[8,4,16,512]{3,2,1,0:T(8,128)S(1)}, f32[8,4,16,512]{3,2,1,0:T(8,128)}, u32[]{:S(2)}) copy-start(f32[8,4,16,512]{3,2,1,0:T(8,128)} %param.3) | copy-start | bytes 3145732
  126.0 2.9 %copy-start.1 = (f32[4,16,8,512]{3,2,1,0:T(8,128)S(1)}, f32[4,16,8,512]{3,2,1,0:T(8,128)}, u32[]{:S(2)}) copy-start(f32[4,16,8,512]{3,2,1,0:T(8,128)} %get-tuple-element.5) | copy-start | bytes 3145732

commit v2 on v1

--- a/solution.py
+++ b/solution.py
@@ -47,7 +47,7 @@
     return upper + pltpu.roll(rest, 8, 1)
 
 
-def kernel(ngx, ngy, X1, Y1, Z, rhs_ref, cf1_ref, sol_ref, res_ref, cf_ref, acc, turn_s, turn_r, back_s, back_r, basis, parts, gs, ag, ar_y, ar_x, send, recv, sy_s, sy_r, sx_s, sx_r):
+def kernel(ngx, ngy, X1, Y1, Z, rhs_ref, vel_ref, rea_ref, sol_ref, res_ref, cf_ref, came, acc, gone, turn_s, turn_r, back_s, back_r, basis, parts, gs, ag, ar_y, ar_x, send, recv, sy_s, sy_r, sx_s, sx_r):
     ix = lax.axis_index("gx")
     iy = lax.axis_index("gy")
     X, Y = 2 * X1, Y1 // 2
@@ -63,10 +63,14 @@
         (jnp.logical_not(upper) | (iy < ngy - 1), jnp.where(upper, ix, partner), jnp.where(upper, iy + 1, iy)),
     ]
 
+    my_rows = pl.ds(pl.multiple_of(half * Y, Y), Y)
+    their_rows = pl.ds(pl.multiple_of((1 - half) * Y, Y), Y)
+
     def swap(which):
         source, target = [
-            (rhs_ref.at[:, pl.ds((1 - half) * Y, Y)], basis.at[0, pl.ds(1 + mine, X1), pl.ds(1, Y)]),
-            (cf1_ref.at[:, pl.ds((1 - half) * Y, Y)], cf_ref.at[pl.ds(mine, X1)]),
+            (rhs_ref.at[:, :, their_rows], came),
+            (vel_ref.at[:, :, their_rows], cf_ref.at[pl.ds(0, 3), pl.ds(mine, X1)]),
+            (rea_ref.at[:, their_rows], cf_ref.at[3, pl.ds(mine, X1)]),
         ][which]
         return pltpu.make_async_remote_copy(
             src_ref=source,
@@ -78,7 +82,7 @@
         )
 
     def swapped(which):
-        target = [basis.at[0, pl.ds(1 + theirs, X1), pl.ds(1, Y)], cf_ref.at[pl.ds(theirs, X1)]][which]
+        target = [came, cf_ref.at[pl.ds(0, 3), pl.ds(theirs, X1)], cf_ref.at[3, pl.ds(theirs, X1)]][which]
         pltpu.make_async_remote_copy(
             src_ref=target,
             dst_ref=target,
@@ -90,8 +94,8 @@
 
     def back(which, plane):
         return pltpu.make_async_remote_copy(
-            src_ref=acc.at[which, theirs + plane],
-            dst_ref=[sol_ref, res_ref][which].at[plane, pl.ds(half * Y, Y)],
+            src_ref=gone.at[which, plane],
+            dst_ref=[sol_ref, res_ref][which].at[:, plane, my_rows],
             send_sem=back_s.at[which, plane],
             recv_sem=back_r.at[which, plane],
             device_id={"gx": partner, "gy": iy},
@@ -99,7 +103,7 @@
         )
 
     def came_back(which, plane):
-        target = [sol_ref, res_ref][which].at[plane, pl.ds((1 - half) * Y, Y)]
+        target = [sol_ref, res_ref][which].at[:, plane, their_rows]
         pltpu.make_async_remote_copy(
             src_ref=target,
             dst_ref=target,
@@ -111,6 +115,7 @@
 
     swap(0).start()
     swap(1).start()
+    swap(2).start()
 
     def face(slot, side):
         return [
@@ -165,6 +170,8 @@
 
     nslots = ITERS * (S + 1)
 
+    gs[...] = jnp.zeros_like(gs)
+
     @pl.loop(0, nslots)
     def _(slot):
         for side in range(4):
@@ -189,7 +196,7 @@
         yp, ym = basis[slot, x, y + 1], basis[slot, x, y - 1]
         zp = jnp.where(last, 0.0, pltpu.roll(c, Z - 1, 1))
         zm = jnp.where(first, 0.0, pltpu.roll(c, 1, 1))
-        cf = [cf_ref[x - 1, y - 1, d : d + 1, :] for d in range(4)]
+        cf = [cf_ref[d, x - 1, y - 1 : y, :] for d in range(4)]
         sums = (xp + xm) - cf[0] * (xp - xm)
         sums = sums + ((yp + ym) - cf[1] * (yp - ym))
         sums = sums + ((zp + zm) - cf[2] * (zp - zm))
@@ -198,15 +205,14 @@
     def inner(slot, power):
         @pl.loop(2, X)
         def _(x):
-            @pl.loop(2, Y, unroll=True)
-            def _(y):
+            for y in range(2, Y):
                 site(slot, power, x, y)
 
     def outer(slot, power):
-        @pl.loop(1, Y + 1, unroll=4)
-        def _(y):
-            site(slot, power, 1, y)
-            site(slot, power, X, y)
+        @pl.loop(0, 2)
+        def _(end):
+            for y in range(1, Y + 1):
+                site(slot, power, 1 + end * (X - 1), y)
 
         @pl.loop(2, X, unroll=True)
         def _(x):
@@ -245,13 +251,22 @@
             to(d).wait_send()
         return total
 
+    low = 16 * S
+
+    def gram_low():
+        def add(at, total):
+            block = parts[at, 0:low]
+            return total + lax.dot_general(block, block, (((1,), (1,)), ((), ())), preferred_element_type=F32)
+
+        gs[0:low, 0:low] = lax.fori_loop(0, X * Y, add, jnp.zeros((low, low), F32), unroll=8)
+
     def gram_of(outer_step):
         def add(at, total):
-            block = parts[at]
-            return total + lax.dot_general(block, block, (((1,), (1,)), ((), ())), preferred_element_type=F32)
-
-        gs[...] = jnp.zeros_like(gs)
-        gs[:, 0:80] = lax.fori_loop(0, X * Y, add, jnp.zeros((80, 80), F32), unroll=8)
+            return total + lax.dot_general(
+                parts[at], parts[at, low : low + 16], (((1,), (1,)), ((), ())), preferred_element_type=F32
+            )
+
+        gs[:, low : low + 16] = lax.fori_loop(0, X * Y, add, jnp.zeros((low + 16, 16), F32), unroll=8)
         rows = jnp.concatenate([gs[16 * j : 16 * j + 8, :] + gs[16 * j + 8 : 16 * j + 16, :] for j in range(S + 1)], axis=0)
         lanes = iota((40, 128), 1)
         gram = jnp.zeros((40, 128), F32)
@@ -264,23 +279,28 @@
         ag[outer_step, 1] = exchange(outer_step, 0, ngy, iy, ar_y, sy_s, sy_r)
         total = exchange(outer_step, 1, ngx, ix, ar_x, sx_s, sx_r)
         gram = jnp.concatenate([total, pltpu.roll(total, 88, 1), pltpu.roll(total, 48, 1)[:8]], axis=0)
-        return jnp.where(lanes < 40, gram, 0.0)
+        gram = jnp.where(lanes < 40, gram, 0.0)
+        turned = jnp.concatenate([gram, jnp.zeros((88, 128), F32)], axis=0).T[32:40]
+        turned = jnp.where(iota((8, 128), 1) < 32, turned, gram[32:40])
+        return jnp.concatenate([gram[:32], turned], axis=0)
+
+    def place(x, fields):
+        turned = jnp.swapaxes(fields, 0, 1)
+        for y in range(Y):
+            keep(0, 0, x + 1, y + 1, turned[y])
 
     @pl.loop(0, X1)
     def _(x):
-        @pl.loop(0, Y, unroll=8)
-        def _(y):
-            keep(0, 0, mine + x + 1, y + 1, rhs_ref[x, half * Y + y])
-            cf_ref[mine + x, y] = cf1_ref[x, half * Y + y]
+        place(mine + x, rhs_ref[:, x, my_rows, :])
+        for d in range(3):
+            cf_ref[d, mine + x] = vel_ref[d, x, my_rows, :]
+        cf_ref[3, mine + x] = rea_ref[x, my_rows, :]
 
     swapped(0)
 
-    def split_swapped():
-        @pl.loop(0, X1)
-        def _(x):
-            @pl.loop(0, Y, unroll=8)
-            def _(y):
-                parts[(theirs + x) * Y + y, pl.ds(0, 16)] = split(basis[0, theirs + x + 1, y + 1])
+    @pl.loop(0, X1)
+    def _(x):
+        place(theirs + x, came[:, x])
 
     for outer_step in range(ITERS):
         base = outer_step * (S + 1)
@@ -292,9 +312,14 @@
             if outer_step == 0:
                 @pl.when(power == 0)
                 def _():
-                    split_swapped()
                     swapped(1)
+                    swapped(2)
             inner(slot, power)
+
+            @pl.when(power == S - 1)
+            def _():
+                gram_low()
+
             wait_recvs(slot)
             outer(slot, power)
             wait_sends(slot)
@@ -310,7 +335,11 @@
         def combined(x, y):
             both = jnp.dot(left, parts[x * Y + y], preferred_element_type=F32)
             sol, res = both[0:8] + both[16:24], both[8:16] + both[24:32]
-            return sol if outer_step == 0 else acc[0, x, y] + sol, res
+            return sol if outer_step == 0 else acc[x, y] + sol, res
+
+        def plane(x):
+            both = [combined(x, y) for y in range(Y)]
+            return tuple(jnp.swapaxes(jnp.stack([one[k] for one in both]), 0, 1) for k in range(2))
 
         if outer_step < ITERS - 1:
             @pl.loop(0, X)
@@ -318,27 +347,24 @@
                 @pl.loop(0, Y, unroll=8)
                 def _(y):
                     sol, res = combined(x, y)
-                    acc[0, x, y] = sol
+                    acc[x, y] = sol
                     keep(base + S + 1, 0, x + 1, y + 1, res)
         else:
             @pl.loop(0, X1)
             def _(x):
-                @pl.loop(0, Y, unroll=8)
-                def _(y):
-                    acc[0, theirs + x, y], acc[1, theirs + x, y] = combined(theirs + x, y)
-
+                sol, res = plane(theirs + x)
+                gone[0, x] = sol
+                gone[1, x] = res
                 back(0, x).start()
                 back(1, x).start()
 
             @pl.loop(0, X1)
             def _(x):
-                @pl.loop(0, Y, unroll=8)
-                def _(y):
-                    sol, res = combined(mine + x, y)
-                    sol_ref[x, half * Y + y] = sol
-                    res_ref[x, half * Y + y] = res
-
-            for which in range(2):
+                sol, res = plane(mine + x)
+                sol_ref[:, x, my_rows, :] = sol
+                res_ref[:, x, my_rows, :] = res
+
+            for which in range(3):
                 swap(which).wait_send()
 
             @pl.loop(0, X1)
@@ -350,21 +376,21 @@
 
 def local(ngx, ngy, right_side, velocity, reaction):
     nrhs, X, Y, Z = right_side.shape
-    rhs = jnp.transpose(right_side, (1, 2, 0, 3))
-    cf = jnp.transpose(jnp.concatenate([velocity, reaction[None]], axis=0), (1, 2, 0, 3))
     nslots = ITERS * (S + 1)
     vmem = pl.BlockSpec(memory_space=pltpu.VMEM)
-    out = jax.ShapeDtypeStruct((X, Y, nrhs, Z), F32)
-    sol, res = pl.pallas_call(
+    out = jax.ShapeDtypeStruct(right_side.shape, F32)
+    return pl.pallas_call(
         functools.partial(kernel, ngx, ngy, X, Y, Z),
         out_shape=(out, out),
-        in_specs=[vmem, vmem],
+        in_specs=[vmem, vmem, vmem],
         out_specs=(vmem, vmem),
         scratch_shapes=[
-            pltpu.VMEM((2 * X, Y // 2, 4, Z), F32),
-            pltpu.VMEM((2, 2 * X, Y // 2, nrhs, Z), F32),
-            pltpu.SemaphoreType.DMA((2,)),
-            pltpu.SemaphoreType.DMA((2,)),
+            pltpu.VMEM((4, 2 * X, Y // 2, Z), F32),
+            pltpu.VMEM((nrhs, X, Y // 2, Z), F32),
+            pltpu.VMEM((2 * X, Y // 2, nrhs, Z), F32),
+            pltpu.VMEM((2, X, nrhs, Y // 2, Z), F32),
+            pltpu.SemaphoreType.DMA((3,)),
+            pltpu.SemaphoreType.DMA((3,)),
             pltpu.SemaphoreType.DMA((2, X)),
             pltpu.SemaphoreType.DMA((2, X)),
             pltpu.VMEM((nslots, 2 * X + 2, Y // 2 + 2, nrhs, Z), F32),
@@ -381,8 +407,7 @@
             pltpu.SemaphoreType.DMA((ITERS, ngx)),
         ],
         compiler_params=pltpu.CompilerParams(has_side_effects=True, vmem_limit_bytes=56 * 1024 * 1024),
-    )(rhs, cf)
-    return jnp.transpose(sol, (2, 0, 1, 3)), jnp.transpose(res, (2, 0, 1, 3))
+    )(right_side, velocity, reaction)
 
 
 def solution(mesh):

time: 131 us -> 124 us (0.947)
  local copies, waits for them, and re-layouts: 8.42 us -> 3.37 us
    unnamed x8 -> x4, local copies, waits for them, and re-layouts: 7.42 us -> 3.37 us
where the time goes in v2:
time: 124 us
  Pallas kernels  120 us (97%)
  local copies, waits for them, and re-layouts  3.37 us (3%)
    pallas_call x1, Pallas kernels, local(): pl.pallas_call(functools.partial(kernel, ngx, ngy, X, Y, Z), out_shape=(o...  120 us
    unnamed x4, local copies, waits for them, and re-layouts  3.37 us

profile of v2, /device:TPU:0, one launch (start us, length us, event | category | flops | bytes accessed | tf_op | source)
XLA Modules:
  0.0 124.3 jit_solution(3050178795352910560)
XLA Ops:
  0.6 120.3 %shard_map.50 = (f32[8,4,16,512]{3,2,1,0:T(8,128)}, f32[8,4,16,512]{3,2,1,0:T(8,128)}) custom-call(f32[8,4,16,512]{3,2,1,0:T(8,128)} %rhs_ref.1, f32[3,4,16,512]{3,2,1,0:T(8,128)} %vel_ref.1, f32[4,16,512]{2,1,0:T(8,128)} %rea_ref.1), custom_call_target="tpu_custom_call" | custom-call | tf_op jit(solution)/shard_map/pallas_call | solution.py:382
  120.9 0.0 copy-start
  120.9 2.4 %copy.7 = f32[8,4,16,512]{3,2,1,0:T(8,128)} copy(f32[8,4,16,512]{3,2,1,0:T(8,128)} %get-tuple-element.4) | data formatting | bytes 2097152
  123.3 0.0 copy-done
  123.3 1.0 copy.8
Async XLA Ops:
  120.9 2.4 %copy-start = (f32[8,4,16,512]{3,2,1,0:T(8,128)S(1)}, f32[8,4,16,512]{3,2,1,0:T(8,128)}, u32[]{:S(2)}) copy-start(f32[8,4,16,512]{3,2,1,0:T(8,128)} %get-tuple-element.5) | copy-start | bytes 3145732
